TPU v7x, 32 devices: a whole 2x2x4 slice. The times are simulated.
32 devices in a mesh: gx: 4 (over y, x), gy: 4 (over z), layer: 2 (over core).
Axes of the slice: x: 2, y: 2, z: 4, core: 2. Of those that a mesh axis runs over, the one named last changes fastest.
Arguments:
- profiles: bfloat16 [2, 4, 65536, 256], P('layer', 'gx', 'gy'), may hold values from 0.049804688 to 2
- time_weight: bfloat16 [256], replicated, may hold values from 0 to 0.029907227
- slot_cell: int32 [2, 4, 65536], P('layer', 'gx', 'gy'), may hold values from 0 to 65535
- inst_count: int32 [2, 4, 4], P('layer', 'gx', 'gy'), may hold values from 1 to 16384, as said below
- metal: float32 [6, 512, 2048], P('layer', 'gx', 'gy'), may hold values from 0.5 to 4
- via_density: float32 [512, 2048], P('gx', 'gy'), may hold values from 0.5 to 4
- pad: float32 [512, 2048], P('gx', 'gy'), may hold values from 0.05 to 0.5
- start_drop: float32 [6, 512, 2048], P('layer', 'gx', 'gy'), may hold values from 0 to 1
Outputs:
- drop: float32 [6, 512, 2048], P('layer', 'gx', 'gy')
- residual: float32 [6, 512, 2048], P('layer', 'gx', 'gy')
Inputs may be any that keep to these rules, and one draw needn't show every extreme that they name: The first inst_count slots of a device are live, the rest are padding; and one device is full in every draw. `slot_cell`: row-major cell index within the tile of 128 x 512 cells.
All inputs are finite; a program needn't handle non-finite values.
Results may differ from a plain program's by a relative error of at most 0.0018.
Values sent between devices are 32-bit elements; how exact they have to be, the bound alone decides.
A program may use at most 64 MiB of HBM per device.

v0:
```python
import jax
import jax.numpy as jnp
from jax import lax
from jax.sharding import PartitionSpec as P

BLOCK = 512
ITERS = 3


def from_behind(value, axis, steps):
    count = lax.axis_size(axis)
    first, last = (max(0, -steps), min(count, count - steps))
    return lax.ppermute(value, axis, [(source, source + steps) for source in range(first, last)])


def with_halo(shard, sides, width):
    for axis, dim in sides:
        devices, length = (lax.axis_size(axis), shard.shape[dim])
        up = [(i, (i + 1) % devices) for i in range(devices - 1)]
        down = [(j, i) for i, j in up]
        last = lax.slice_in_dim(shard, length - width, length, axis=dim)
        first = lax.slice_in_dim(shard, 0, width, axis=dim)
        before = lax.ppermute(last, axis, up)
        after = lax.ppermute(first, axis, down)
        shard = jnp.concatenate([before, shard, after], axis=dim)
    return shard


def harmonic(values, beside):
    return 2.0 * values * beside / (values + beside)


def links(extended, via_column):
    middle = extended[1:-1, 1:-1, 1:-1]
    east_link = harmonic(middle, extended[1:-1, 2:, 1:-1])
    west_link = harmonic(middle, extended[1:-1, :-2, 1:-1])
    north_link = harmonic(middle, extended[1:-1, 1:-1, 2:])
    south_link = harmonic(middle, extended[1:-1, 1:-1, :-2])
    upper_link = via_column * harmonic(middle, extended[2:, 1:-1, 1:-1])
    lower_link = via_column * harmonic(middle, extended[:-2, 1:-1, 1:-1])
    return (east_link, west_link, north_link, south_link, upper_link, lower_link)


def diagonal_of(conduct):
    east_link, west_link, north_link, south_link, upper_link, lower_link = conduct
    return east_link + west_link + north_link + south_link + upper_link + lower_link


def operate(field, extended, conduct, diagonal):
    east_link, west_link, north_link, south_link, upper_link, lower_link = conduct
    result = (
        diagonal * field
        - east_link * extended[1:-1, 2:, 1:-1]
        - west_link * extended[1:-1, :-2, 1:-1]
    )
    result = result - north_link * extended[1:-1, 1:-1, 2:] - south_link * extended[1:-1, 1:-1, :-2]
    return result - upper_link * extended[2:, 1:-1, 1:-1] - lower_link * extended[:-2, 1:-1, 1:-1]


def both_sums(residual, scaled, image):
    return lax.psum((jnp.sum(residual * scaled), jnp.sum(scaled * image)), ("gx", "gy", "layer"))


def solve(apply, diagonal, rhs, start):
    solution = start
    residual = rhs - apply(start)
    scaled = residual / diagonal
    image = apply(scaled)
    energy, curvature = both_sums(residual, scaled, image)
    step_size = energy / curvature
    direction, along = (scaled, image)
    for iteration in range(ITERS):
        solution = solution + step_size * direction
        residual = residual - step_size * along
        if iteration + 1 < ITERS:
            scaled = residual / diagonal
            image = apply(scaled)
            energy_next, curvature = both_sums(residual, scaled, image)
            momentum = energy_next / energy
            step_size = energy_next / (curvature - momentum * energy_next / step_size)
            direction = scaled + momentum * direction
            along = image + momentum * along
            energy = energy_next
    return (solution, residual)


def per_device(profiles, time_weight, slot_cell, inst_count, metal, via_density, pad, start_drop):
    tile_rows, tile_cols = (metal.shape[1], metal.shape[2])
    slot_current = jnp.dot(
        profiles.reshape(-1, profiles.shape[-1]), time_weight, preferred_element_type=jnp.float32
    )
    slot_cells = slot_cell.reshape(-1)
    live_count = inst_count.reshape(())
    positions = jnp.arange(slot_cells.shape[0], dtype=jnp.int32)
    slot_current = jnp.where(positions < live_count, slot_current, 0.0)
    block_rows = min(BLOCK, slot_cells.shape[0])
    blocks_live = (live_count + block_rows - 1) // block_rows
    row_ids = jnp.arange(tile_rows, dtype=jnp.int32)
    col_ids = jnp.arange(tile_cols, dtype=jnp.int32)

    def add_block(block_index, total):
        first = block_index * block_rows
        cells = lax.dynamic_slice_in_dim(slot_cells, first, block_rows)
        amounts = lax.dynamic_slice_in_dim(slot_current, first, block_rows)
        left = jnp.where(cells[:, None] // tile_cols == row_ids[None, :], amounts[:, None], 0.0)
        left_high = left.astype(jnp.bfloat16)
        left_low = (left - left_high.astype(jnp.float32)).astype(jnp.bfloat16)
        right = (cells[:, None] % tile_cols == col_ids[None, :]).astype(jnp.bfloat16)
        dims = (((0,), (0,)), ((), ()))
        upper_part = lax.dot_general(left_high, right, dims, preferred_element_type=jnp.float32)
        lower_part = lax.dot_general(left_low, right, dims, preferred_element_type=jnp.float32)
        return total + (upper_part + lower_part)

    partial_value = lax.fori_loop(
        0, blocks_live, add_block, jnp.zeros((tile_rows, tile_cols), jnp.float32)
    )
    others = from_behind(partial_value, "layer", -1)
    bottom = lax.axis_index("layer") == 0
    current = jnp.where(bottom, partial_value + others, 0.0)
    rhs = jnp.zeros_like(metal).at[0].set(current)
    extended = with_halo(metal, (("gx", 1), ("gy", 2), ("layer", 0)), 1)
    conduct = links(extended, via_density[None])
    top = lax.axis_index("layer") == lax.axis_size("layer") - 1
    diagonal = diagonal_of(conduct).at[-1].add(jnp.where(top, pad, 0.0))

    def apply(field):
        rims = with_halo(field, (("gx", 1), ("gy", 2), ("layer", 0)), 1)
        return operate(field, rims, conduct, diagonal)

    solution, residual = solve(apply, diagonal, rhs, start_drop)
    return (solution, residual)


def solution(mesh):
    in_specs = (
        P("layer", "gx", "gy", None),
        P(),
        P("layer", "gx", "gy"),
        P("layer", "gx", "gy"),
        P("layer", "gx", "gy"),
        P("gx", "gy"),
        P("gx", "gy"),
        P("layer", "gx", "gy"),
    )
    out_specs = (P("layer", "gx", "gy"), P("layer", "gx", "gy"))
    return jax.shard_map(
        per_device, mesh=mesh, in_specs=in_specs, out_specs=out_specs, check_vma=False
    )
```

profile of v0, /device:TPU:0, one launch (start us, length us, event | category | flops | bytes accessed | tf_op | source)
XLA Modules:
  0.0 358.4 jit_solution(6183316675431380486)
XLA Ops:
  1.5 4.9 %collective-permute-start.2 = (f32[3,1,512]{2,1,0:T(1,128)S(1)}, f32[3,1,512]{2,1,0:T(1,128)S(1)}, u32[]{:S(2)}, u32[]{:S(2)}) collective-permute-start(f32[3,1,512]{2,1,0:T(1,128)S(1)} %get-tuple-element.200), channel_id=1, source_target_pairs={{0,8},{8,16},{16,24},{1,9},{9,17},{17,25},{2,10},{10,18},{18,26},{... | collective-permute-start | bytes 18440 | tf_op jit(solution)/shard_map/ppermute | solution.py:23
  6.3 1.3 collective-permute-start.1
  8.5 4.5 %collective-permute-start.8 = (f32[3,1,512]{2,1,0:T(1,128)S(1)}, f32[3,1,512]{2,1,0:T(1,128)S(1)}, u32[]{:S(2)}, u32[]{:S(2)}) collective-permute-start(f32[3,1,512]{2,1,0:T(1,128)S(1)} %get-tuple-element.198), channel_id=1, source_target_pairs={{0,8},{8,16},{16,24},{1,9},{9,17},{17,25},{2,10},{10,18},{18,26},{... | collective-permute-start | bytes 18440 | tf_op jit(solution)/shard_map/ppermute | solution.py:23
  13.0 1.3 collective-permute-start.7
  15.7 5.8 %fusion.19 = f32[1,16384]{1,0:T(1,128)S(1)} fusion(bf16[256,1]{0,1:T(2,128)(2,1)S(1)} %reshape.111, bf16[1,1,16384,256]{3,2,1,0:T(8,128)(2,1)} %param.14), kind=kOutput, calls=%fused_computation.28 | convolution fusion | flops 8388608 | bytes 8454656 | tf_op jit(solution)/shard_map/dot_general | solution.py:89
  21.5 12.7 %while.15 = (s32[]{:T(128)}, f32[128,512]{1,0:T(8,128)S(1)}, s32[]{:T(128)}, s32[16384]{0:T(1024)}, f32[16384]{0:T(1024)S(1)}, /*index=5*/s32[]{:T(128)}, s32[]{:T(128)}, s32[]{:T(128)}, s32[]{:T(128)}) while((s32[]{:T(128)}, f32[128,512]{1,0:T(8,128)S(1)}, s32[]{:T(128)}, s32[16384]{0:T(1024)}, f32[16384]{0:T(1024)S(1)}, ...), condition=%wide.region_1.2_spmd.clone, body=%wide.region_0.1_spmd.clone.sunk | while | flops 135407104 | bytes 1071251 | solution.py:114
  34.2 1.3 collective-permute-start
  35.7 22.6 %collective-permute-start.4 = (f32[3,130,1]{2,1,0:T(8,128)S(1)}, f32[3,130,1]{2,1,0:T(8,128)S(1)}, u32[]{:S(2)}, u32[]{:S(2)}) collective-permute-start(f32[3,130,1]{2,1,0:T(8,128)S(1)} %get-tuple-element.190), channel_id=1, source_target_pairs={{0,2},{2,4},{4,6},{1,3},{3,5},{5,7},{8,10},{10,12},{12,14},{9,11},... | collective-permute-start | bytes 4688 | tf_op jit(solution)/shard_map/ppermute | solution.py:23
  58.3 1.3 collective-permute-start.3
  59.8 21.1 %collective-permute-start.10 = (f32[3,130,1]{2,1,0:T(8,128)S(1)}, f32[3,130,1]{2,1,0:T(8,128)S(1)}, u32[]{:S(2)}, u32[]{:S(2)}) collective-permute-start(f32[3,130,1]{2,1,0:T(8,128)S(1)} %get-tuple-element.188), channel_id=1, source_target_pairs={{0,2},{2,4},{4,6},{1,3},{3,5},{5,7},{8,10},{10,12},{12,14},{9,11},... | collective-permute-start | bytes 4688 | tf_op jit(solution)/shard_map/ppermute | solution.py:23
  80.9 1.3 collective-permute-start.9
  82.2 2.4 collective-permute-done.3
  84.9 2.0 collective-permute-start.6
  87.0 1.3 collective-permute-start.5
  88.3 21.1 %collective-permute-done.9 = f32[3,130,1]{2,1,0:T(8,128)S(1)} collective-permute-done((f32[3,130,1]{2,1,0:T(8,128)S(1)}, f32[3,130,1]{2,1,0:T(8,128)S(1)}, u32[]{:S(2)}, u32[]{:S(2)}) %collective-permute-start.9) | collective-permute-done | bytes 1592 | tf_op jit(solution)/shard_map/ppermute | solution.py:24
  109.7 1.3 collective-permute-start.11
  111.0 3.1 collective-permute-start.12
  114.1 3.5 add_add_fusion
  117.8 3.7 %fusion.83 = (f32[3,128,512]{2,1,0:T(8,128)S(1)}, f32[3,128,512]{2,1,0:T(8,128)S(1)}) fusion(f32[3,128,512]{2,1,0:T(8,128)S(1)} %fusion.76, f32[3,128,512]{2,1,0:T(8,128)S(1)} %get-tuple-element.169, f32[3,130,1]{2,1,0:T(8,128)S(1)} %collective-permute-done.9, f32[3,1,512]{2,1,0:T(1,128)S(1)} %collective-permute-done.7, f32[3,128,512]{2,1,0:T(8,128)S(1)} %copy-done.6, ...), kind=kLoop, calls=%fused_computation.238 | loop fusion | flops 10616832 | bytes 6332544 | tf_op jit(solution)/shard_map/div | solution.py:67
  124.2 8.7 %collective-permute-done.13 = f32[3,1,512]{2,1,0:T(1,128)S(1)} collective-permute-done((f32[3,1,512]{2,1,0:T(1,128)S(1)}, f32[3,1,512]{2,1,0:T(1,128)S(1)}, u32[]{:S(2)}, u32[]{:S(2)}) %collective-permute-start.13) | collective-permute-done | bytes 6176 | tf_op jit(solution)/shard_map/ppermute | solution.py:24
  133.1 3.7 %collective-permute-start.16 = (f32[3,130,1]{2,1,0:T(8,128)S(1)}, f32[3,130,1]{2,1,0:T(8,128)S(1)}, u32[]{:S(2)}, u32[]{:S(2)}) collective-permute-start(f32[3,130,1]{2,1,0:T(8,128)S(1)} %get-tuple-element.186), channel_id=1, source_target_pairs={{0,2},{2,4},{4,6},{1,3},{3,5},{5,7},{8,10},{10,12},{12,14},{9,11},... | collective-permute-start | bytes 4688 | tf_op jit(solution)/shard_map/ppermute | solution.py:23
  138.0 2.6 collective-permute-done.16
  140.6 4.1 %collective-permute-done.15 = f32[3,130,1]{2,1,0:T(8,128)S(1)} collective-permute-done((f32[3,130,1]{2,1,0:T(8,128)S(1)}, f32[3,130,1]{2,1,0:T(8,128)S(1)}, u32[]{:S(2)}, u32[]{:S(2)}) %collective-permute-start.15) | collective-permute-done | bytes 1592 | tf_op jit(solution)/shard_map/ppermute | solution.py:24
  146.4 3.1 collective-permute-start.18
  150.7 5.0 %multiply_reduce_fusion.4 = (f32[]{:T(128)}, f32[]{:T(128)}, f32[3,128,512]{2,1,0:T(8,128)}) fusion(f32[3,128,512]{2,1,0:T(8,128)S(1)} %get-tuple-element.165, f32[3,128,512]{2,1,0:T(8,128)S(1)} %get-tuple-element.166, f32[3,128,512]{2,1,0:T(8,128)S(1)} %get-tuple-element.169, f32[3,130,1]{2,1,0:T(8,128)S(1)} %collective-permute-done.15, ...), kind=kLoop, calls=%fused_computation.184 | loop fusion | flops 11010046 | bytes 6070408 | tf_op jit(solution)/shard_map/reduce_sum | solution.py:61
  155.7 40.6 %all-reduce.3 = (f32[]{:T(128)}, f32[]{:T(128)}) all-reduce(f32[]{:T(128)} %get-tuple-element.141, f32[]{:T(128)} %get-tuple-element.140), channel_id=1, replica_groups=mesh['gx'=4,'gy'=4,'layer'=2] {'gx','gy','layer'}, use_global_device_ids=true, to_apply=%region_3.4 | all-reduce | flops 2 | bytes 16 | tf_op jit(solution)/shard_map/psum | solution.py:61
  197.6 1.7 fusion.81
  199.3 4.2 %collective-permute-start.20 = (f32[3,1,512]{2,1,0:T(1,128)S(1)}, f32[3,1,512]{2,1,0:T(1,128)S(1)}, u32[]{:S(2)}, u32[]{:S(2)}) collective-permute-start(f32[3,1,512]{2,1,0:T(1,128)S(1)} %get-tuple-element.194), channel_id=1, source_target_pairs={{0,8},{8,16},{16,24},{1,9},{9,17},{17,25},{2,10},{10,18},{18,26},{... | collective-permute-start | bytes 18440 | tf_op jit(solution)/shard_map/ppermute | solution.py:23
  203.5 1.3 collective-permute-start.19
  204.9 4.2 %collective-permute-done.19 = f32[3,1,512]{2,1,0:T(1,128)S(1)} collective-permute-done((f32[3,1,512]{2,1,0:T(1,128)S(1)}, f32[3,1,512]{2,1,0:T(1,128)S(1)}, u32[]{:S(2)}, u32[]{:S(2)}) %collective-permute-start.19) | collective-permute-done | bytes 6176 | tf_op jit(solution)/shard_map/ppermute | solution.py:24
  209.2 2.2 collective-permute-start.22
  212.7 2.0 collective-permute-done.22
  214.7 4.4 %collective-permute-done.21 = f32[3,130,1]{2,1,0:T(8,128)S(1)} collective-permute-done((f32[3,130,1]{2,1,0:T(8,128)S(1)}, f32[3,130,1]{2,1,0:T(8,128)S(1)}, u32[]{:S(2)}, u32[]{:S(2)}) %collective-permute-start.21) | collective-permute-done | bytes 1592 | tf_op jit(solution)/shard_map/ppermute | solution.py:24
  219.4 1.5 collective-permute-start.23
  220.9 3.1 collective-permute-start.24
  225.2 6.3 %multiply_reduce_fusion.2 = (f32[]{:T(128)}, f32[]{:T(128)}, f32[3,128,512]{2,1,0:T(8,128)}) fusion(f32[3,128,512]{2,1,0:T(8,128)S(1)} %get-tuple-element.162, f32[3,128,512]{2,1,0:T(8,128)S(1)} %get-tuple-element.163, f32[3,128,512]{2,1,0:T(8,128)} %copy-done.4, f32[3,130,1]{2,1,0:T(8,128)S(1)} %collective-permute-done.21, ...), kind=kLoop, calls=%fused_computation.181 | loop fusion | flops 11010046 | bytes 6070408 | tf_op jit(solution)/shard_map/reduce_sum | solution.py:61
  231.5 39.9 %all-reduce.2 = (f32[]{:T(128)}, f32[]{:T(128)}) all-reduce(f32[]{:T(128)} %get-tuple-element.139, f32[]{:T(128)} %get-tuple-element.138), channel_id=1, replica_groups=mesh['gx'=4,'gy'=4,'layer'=2] {'gx','gy','layer'}, use_global_device_ids=true, to_apply=%region_7.8 | all-reduce | flops 2 | bytes 16 | tf_op jit(solution)/shard_map/psum | solution.py:61
  275.9 2.1 fusion.79
  278.0 4.2 %collective-permute-start.26 = (f32[3,1,512]{2,1,0:T(1,128)S(1)}, f32[3,1,512]{2,1,0:T(1,128)S(1)}, u32[]{:S(2)}, u32[]{:S(2)}) collective-permute-start(f32[3,1,512]{2,1,0:T(1,128)S(1)} %get-tuple-element.192), channel_id=1, source_target_pairs={{0,8},{8,16},{16,24},{1,9},{9,17},{17,25},{2,10},{10,18},{18,26},{... | collective-permute-start | bytes 18440 | tf_op jit(solution)/shard_map/ppermute | solution.py:23
  282.2 1.3 collective-permute-start.25
  283.6 4.2 %collective-permute-done.25 = f32[3,1,512]{2,1,0:T(1,128)S(1)} collective-permute-done((f32[3,1,512]{2,1,0:T(1,128)S(1)}, f32[3,1,512]{2,1,0:T(1,128)S(1)}, u32[]{:S(2)}, u32[]{:S(2)}) %collective-permute-start.25) | collective-permute-done | bytes 6176 | tf_op jit(solution)/shard_map/ppermute | solution.py:24
  287.9 3.0 collective-permute-start.28
  292.2 2.0 collective-permute-done.28
  294.1 4.4 %collective-permute-done.27 = f32[3,130,1]{2,1,0:T(8,128)S(1)} collective-permute-done((f32[3,130,1]{2,1,0:T(8,128)S(1)}, f32[3,130,1]{2,1,0:T(8,128)S(1)}, u32[]{:S(2)}, u32[]{:S(2)}) %collective-permute-start.27) | collective-permute-done | bytes 1592 | tf_op jit(solution)/shard_map/ppermute | solution.py:24
  300.2 3.1 collective-permute-start.30
  304.5 6.0 %multiply_reduce_fusion = (f32[]{:T(128)}, f32[]{:T(128)}, f32[3,128,512]{2,1,0:T(8,128)}) fusion(f32[3,128,512]{2,1,0:T(8,128)S(1)} %get-tuple-element.159, f32[3,128,512]{2,1,0:T(8,128)S(1)} %get-tuple-element.160, f32[3,128,512]{2,1,0:T(8,128)S(1)} %copy-done.5, f32[3,130,1]{2,1,0:T(8,128)S(1)} %collective-permute-done.27, ...), kind=kLoop, calls=%fused_computation.177 | loop fusion | flops 11010046 | bytes 6070408 | tf_op jit(solution)/shard_map/reduce_sum | solution.py:61
  310.5 39.9 %all-reduce.1 = (f32[]{:T(128)}, f32[]{:T(128)}) all-reduce(f32[]{:T(128)} %get-tuple-element.137, f32[]{:T(128)} %get-tuple-element.136), channel_id=1, replica_groups=mesh['gx'=4,'gy'=4,'layer'=2] {'gx','gy','layer'}, use_global_device_ids=true, to_apply=%region_11.12 | all-reduce | flops 2 | bytes 16 | tf_op jit(solution)/shard_map/psum | solution.py:61
  354.2 4.2 %multiply_subtract_fusion = (f32[3,128,512]{2,1,0:T(8,128)}, f32[3,128,512]{2,1,0:T(8,128)}) fusion(f32[3,128,512]{2,1,0:T(8,128)} %copy-done.8, f32[3,128,512]{2,1,0:T(8,128)} %get-tuple-element.158, f32[]{:T(128)S(6)} %div.84, f32[]{:T(128)S(6)} %div.86, f32[3,128,512]{2,1,0:T(8,128)} %get-tuple-element.161, f32[3,128,512]{2,1,0:T(8,128)} %get-tuple-element.164, ...), kind=kLoop, calls=%fused_computation.175 | loop fusion | flops 3145728 | bytes 7864340 | tf_op jit(solution)/shard_map/sub | solution.py:74
  (93 shorter events, 30.2 us)
Async XLA Ops:
  1.5 34.1 %collective-permute-start.2 = (f32[3,1,512]{2,1,0:T(1,128)S(1)}, f32[3,1,512]{2,1,0:T(1,128)S(1)}, u32[]{:S(2)}, u32[]{:S(2)}) collective-permute-start(f32[3,1,512]{2,1,0:T(1,128)S(1)} %get-tuple-element.200), channel_id=1, source_target_pairs={{0,8},{8,16},{16,24},{1,9},{9,17},{17,25},{2,10},{10,18},{18,26},{... | collective-permute-start | bytes 18440 | tf_op jit(solution)/shard_map/ppermute | solution.py:23
  6.3 29.2 %collective-permute-start.1 = (f32[3,1,512]{2,1,0:T(1,128)S(1)}, f32[3,1,512]{2,1,0:T(1,128)S(1)}, u32[]{:S(2)}, u32[]{:S(2)}) collective-permute-start(f32[3,1,512]{2,1,0:T(1,128)S(1)} %get-tuple-element.201), channel_id=1, source_target_pairs={{8,0},{16,8},{24,16},{9,1},{17,9},{25,17},{10,2},{18,10},{26,18},{... | collective-permute-start | bytes 18440 | tf_op jit(solution)/shard_map/ppermute | solution.py:24
  8.5 51.1 %collective-permute-start.8 = (f32[3,1,512]{2,1,0:T(1,128)S(1)}, f32[3,1,512]{2,1,0:T(1,128)S(1)}, u32[]{:S(2)}, u32[]{:S(2)}) collective-permute-start(f32[3,1,512]{2,1,0:T(1,128)S(1)} %get-tuple-element.198), channel_id=1, source_target_pairs={{0,8},{8,16},{16,24},{1,9},{9,17},{17,25},{2,10},{10,18},{18,26},{... | collective-permute-start | bytes 18440 | tf_op jit(solution)/shard_map/ppermute | solution.py:23
  13.0 46.6 %collective-permute-start.7 = (f32[3,1,512]{2,1,0:T(1,128)S(1)}, f32[3,1,512]{2,1,0:T(1,128)S(1)}, u32[]{:S(2)}, u32[]{:S(2)}) collective-permute-start(f32[3,1,512]{2,1,0:T(1,128)S(1)} %get-tuple-element.199), channel_id=1, source_target_pairs={{8,0},{16,8},{24,16},{9,1},{17,9},{25,17},{10,2},{18,10},{26,18},{... | collective-permute-start | bytes 18440 | tf_op jit(solution)/shard_map/ppermute | solution.py:24
  15.7 19.9 %copy-start = (f32[3,128,512]{2,1,0:T(8,128)S(1)}, f32[3,128,512]{2,1,0:T(8,128)}, u32[]{:S(2)}) copy-start(f32[3,128,512]{2,1,0:T(8,128)} %param.18) | copy-start | bytes 2359300
  15.7 44.0 %copy-start.6 = (f32[3,128,512]{2,1,0:T(8,128)S(1)}, f32[3,128,512]{2,1,0:T(8,128)}, u32[]{:S(2)}) copy-start(f32[3,128,512]{2,1,0:T(8,128)} %param.21) | copy-start | bytes 2359300
  34.2 79.8 %collective-permute-start = (f32[128,512]{1,0:T(8,128)S(1)}, f32[128,512]{1,0:T(8,128)S(1)}, u32[]{:S(2)}, u32[]{:S(2)}) collective-permute-start(f32[128,512]{1,0:T(8,128)S(1)} %get-tuple-element.121), channel_id=1, source_target_pairs={{1,0},{3,2},{5,4},{7,6},{9,8},{11,10},{13,12},{15,14},{17,16},{19,... | collective-permute-start | bytes 786440 | tf_op jit(solution)/shard_map/ppermute | solution.py:13
  35.7 46.5 %collective-permute-start.4 = (f32[3,130,1]{2,1,0:T(8,128)S(1)}, f32[3,130,1]{2,1,0:T(8,128)S(1)}, u32[]{:S(2)}, u32[]{:S(2)}) collective-permute-start(f32[3,130,1]{2,1,0:T(8,128)S(1)} %get-tuple-element.190), channel_id=1, source_target_pairs={{0,2},{2,4},{4,6},{1,3},{3,5},{5,7},{8,10},{10,12},{12,14},{9,11},... | collective-permute-start | bytes 4688 | tf_op jit(solution)/shard_map/ppermute | solution.py:23
  58.3 26.3 %collective-permute-start.3 = (f32[3,130,1]{2,1,0:T(8,128)S(1)}, f32[3,130,1]{2,1,0:T(8,128)S(1)}, u32[]{:S(2)}, u32[]{:S(2)}) collective-permute-start(f32[3,130,1]{2,1,0:T(8,128)S(1)} %get-tuple-element.191), channel_id=1, source_target_pairs={{2,0},{4,2},{6,4},{3,1},{5,3},{7,5},{10,8},{12,10},{14,12},{11,9},... | collective-permute-start | bytes 4688 | tf_op jit(solution)/shard_map/ppermute | solution.py:24
  59.8 28.5 %collective-permute-start.10 = (f32[3,130,1]{2,1,0:T(8,128)S(1)}, f32[3,130,1]{2,1,0:T(8,128)S(1)}, u32[]{:S(2)}, u32[]{:S(2)}) collective-permute-start(f32[3,130,1]{2,1,0:T(8,128)S(1)} %get-tuple-element.188), channel_id=1, source_target_pairs={{0,2},{2,4},{4,6},{1,3},{3,5},{5,7},{8,10},{10,12},{12,14},{9,11},... | collective-permute-start | bytes 4688 | tf_op jit(solution)/shard_map/ppermute | solution.py:23
  80.9 28.5 %collective-permute-start.9 = (f32[3,130,1]{2,1,0:T(8,128)S(1)}, f32[3,130,1]{2,1,0:T(8,128)S(1)}, u32[]{:S(2)}, u32[]{:S(2)}) collective-permute-start(f32[3,130,1]{2,1,0:T(8,128)S(1)} %get-tuple-element.189), channel_id=1, source_target_pairs={{2,0},{4,2},{6,4},{3,1},{5,3},{7,5},{10,8},{12,10},{14,12},{11,9},... | collective-permute-start | bytes 4688 | tf_op jit(solution)/shard_map/ppermute | solution.py:24
  84.6 66.1 %copy-start.7 = (f32[3,130,1]{2,1,0:T(8,128)}, f32[3,130,1]{2,1,0:T(8,128)S(1)}, u32[]{:S(2)}) copy-start(f32[3,130,1]{2,1,0:T(8,128)S(1)} %collective-permute-done.3) | copy-start | bytes 4684
  84.9 29.2 %collective-permute-start.6 = (f32[1,130,514]{2,1,0:T(8,128)S(1)}, f32[1,130,514]{2,1,0:T(8,128)S(1)}, u32[]{:S(2)}, u32[]{:S(2)}) collective-permute-start(f32[1,130,514]{2,1,0:T(8,128)S(1)} %get-tuple-element.180), channel_id=1, source_target_pairs={{0,1},{2,3},{4,5},{6,7},{8,9},{10,11},{12,13},{14,15},{16,17},{18,... | collective-permute-start | bytes 801848 | tf_op jit(solution)/shard_map/ppermute | solution.py:23
  87.0 27.1 %collective-permute-start.5 = (f32[1,130,514]{2,1,0:T(8,128)S(1)}, f32[1,130,514]{2,1,0:T(8,128)S(1)}, u32[]{:S(2)}, u32[]{:S(2)}) collective-permute-start(f32[1,130,514]{2,1,0:T(8,128)S(1)} %get-tuple-element.181), channel_id=1, source_target_pairs={{1,0},{3,2},{5,4},{7,6},{9,8},{11,10},{13,12},{15,14},{17,16},{19,... | collective-permute-start | bytes 801848 | tf_op jit(solution)/shard_map/ppermute | solution.py:24
  109.7 8.1 %collective-permute-start.11 = (f32[1,130,514]{2,1,0:T(8,128)S(1)}, f32[1,130,514]{2,1,0:T(8,128)S(1)}, u32[]{:S(2)}, u32[]{:S(2)}) collective-permute-start(f32[1,130,514]{2,1,0:T(8,128)S(1)} %get-tuple-element.178), channel_id=1, source_target_pairs={{1,0},{3,2},{5,4},{7,6},{9,8},{11,10},{13,12},{15,14},{17,16},{19,... | collective-permute-start | bytes 801848 | tf_op jit(solution)/shard_map/ppermute | solution.py:24
  111.0 6.8 %collective-permute-start.12 = (f32[1,130,514]{2,1,0:T(8,128)S(1)}, f32[1,130,514]{2,1,0:T(8,128)S(1)}, u32[]{:S(2)}, u32[]{:S(2)}) collective-permute-start(f32[1,130,514]{2,1,0:T(8,128)S(1)} %get-tuple-element.179), channel_id=1, source_target_pairs={{0,1},{2,3},{4,5},{6,7},{8,9},{10,11},{12,13},{14,15},{16,17},{18,... | collective-permute-start | bytes 801848 | tf_op jit(solution)/shard_map/ppermute | solution.py:23
  117.6 38.1 %copy-start.2 = (f32[3,128,512]{2,1,0:T(8,128)}, f32[3,128,512]{2,1,0:T(8,128)S(1)}, u32[]{:S(2)}) copy-start(f32[3,128,512]{2,1,0:T(8,128)S(1)} %get-tuple-element.168) | copy-start | bytes 2359300
  117.6 38.1 %copy-start.4 = (f32[3,128,512]{2,1,0:T(8,128)}, f32[3,128,512]{2,1,0:T(8,128)S(1)}, u32[]{:S(2)}) copy-start(f32[3,128,512]{2,1,0:T(8,128)S(1)} %get-tuple-element.169) | copy-start | bytes 2359300
  121.5 34.2 %copy-start.10 = (f32[3,128,512]{2,1,0:T(8,128)}, f32[3,128,512]{2,1,0:T(8,128)S(1)}, u32[]{:S(2)}) copy-start(f32[3,128,512]{2,1,0:T(8,128)S(1)} %get-tuple-element.166) | copy-start | bytes 2359300
  121.5 2.6 collective-permute-start.14
  122.8 10.1 %collective-permute-start.13 = (f32[3,1,512]{2,1,0:T(1,128)S(1)}, f32[3,1,512]{2,1,0:T(1,128)S(1)}, u32[]{:S(2)}, u32[]{:S(2)}) collective-permute-start(f32[3,1,512]{2,1,0:T(1,128)S(1)} %get-tuple-element.197), channel_id=1, source_target_pairs={{8,0},{16,8},{24,16},{9,1},{17,9},{25,17},{10,2},{18,10},{26,18},{... | collective-permute-start | bytes 18440 | tf_op jit(solution)/shard_map/ppermute | solution.py:24
  133.1 7.6 %collective-permute-start.16 = (f32[3,130,1]{2,1,0:T(8,128)S(1)}, f32[3,130,1]{2,1,0:T(8,128)S(1)}, u32[]{:S(2)}, u32[]{:S(2)}) collective-permute-start(f32[3,130,1]{2,1,0:T(8,128)S(1)} %get-tuple-element.186), channel_id=1, source_target_pairs={{0,2},{2,4},{4,6},{1,3},{3,5},{5,7},{8,10},{10,12},{12,14},{9,11},... | collective-permute-start | bytes 4688 | tf_op jit(solution)/shard_map/ppermute | solution.py:23
  136.7 8.0 %collective-permute-start.15 = (f32[3,130,1]{2,1,0:T(8,128)S(1)}, f32[3,130,1]{2,1,0:T(8,128)S(1)}, u32[]{:S(2)}, u32[]{:S(2)}) collective-permute-start(f32[3,130,1]{2,1,0:T(8,128)S(1)} %get-tuple-element.187), channel_id=1, source_target_pairs={{2,0},{4,2},{6,4},{3,1},{5,3},{7,5},{10,8},{12,10},{14,12},{11,9},... | collective-permute-start | bytes 4688 | tf_op jit(solution)/shard_map/ppermute | solution.py:24
  145.1 4.4 %collective-permute-start.17 = (f32[1,130,514]{2,1,0:T(8,128)S(1)}, f32[1,130,514]{2,1,0:T(8,128)S(1)}, u32[]{:S(2)}, u32[]{:S(2)}) collective-permute-start(f32[1,130,514]{2,1,0:T(8,128)S(1)} %get-tuple-element.176), channel_id=1, source_target_pairs={{1,0},{3,2},{5,4},{7,6},{9,8},{11,10},{13,12},{15,14},{17,16},{19,... | collective-permute-start | bytes 801848 | tf_op jit(solution)/shard_map/ppermute | solution.py:24
  146.4 4.3 %collective-permute-start.18 = (f32[1,130,514]{2,1,0:T(8,128)S(1)}, f32[1,130,514]{2,1,0:T(8,128)S(1)}, u32[]{:S(2)}, u32[]{:S(2)}) collective-permute-start(f32[1,130,514]{2,1,0:T(8,128)S(1)} %get-tuple-element.177), channel_id=1, source_target_pairs={{0,1},{2,3},{4,5},{6,7},{8,9},{10,11},{12,13},{14,15},{16,17},{18,... | collective-permute-start | bytes 801848 | tf_op jit(solution)/shard_map/ppermute | solution.py:23
  199.3 25.9 %copy-start.9 = (f32[3,128,512]{2,1,0:T(8,128)}, f32[3,128,512]{2,1,0:T(8,128)S(1)}, u32[]{:S(2)}) copy-start(f32[3,128,512]{2,1,0:T(8,128)S(1)} %get-tuple-element.163) | copy-start | bytes 2359300
  199.3 5.5 %collective-permute-start.20 = (f32[3,1,512]{2,1,0:T(1,128)S(1)}, f32[3,1,512]{2,1,0:T(1,128)S(1)}, u32[]{:S(2)}, u32[]{:S(2)}) collective-permute-start(f32[3,1,512]{2,1,0:T(1,128)S(1)} %get-tuple-element.194), channel_id=1, source_target_pairs={{0,8},{8,16},{16,24},{1,9},{9,17},{17,25},{2,10},{10,18},{18,26},{... | collective-permute-start | bytes 18440 | tf_op jit(solution)/shard_map/ppermute | solution.py:23
  203.5 5.5 %collective-permute-start.19 = (f32[3,1,512]{2,1,0:T(1,128)S(1)}, f32[3,1,512]{2,1,0:T(1,128)S(1)}, u32[]{:S(2)}, u32[]{:S(2)}) collective-permute-start(f32[3,1,512]{2,1,0:T(1,128)S(1)} %get-tuple-element.195), channel_id=1, source_target_pairs={{8,0},{16,8},{24,16},{9,1},{17,9},{25,17},{10,2},{18,10},{26,18},{... | collective-permute-start | bytes 18440 | tf_op jit(solution)/shard_map/ppermute | solution.py:24
  209.2 5.5 %collective-permute-start.22 = (f32[3,130,1]{2,1,0:T(8,128)S(1)}, f32[3,130,1]{2,1,0:T(8,128)S(1)}, u32[]{:S(2)}, u32[]{:S(2)}) collective-permute-start(f32[3,130,1]{2,1,0:T(8,128)S(1)} %get-tuple-element.184), channel_id=1, source_target_pairs={{0,2},{2,4},{4,6},{1,3},{3,5},{5,7},{8,10},{10,12},{12,14},{9,11},... | collective-permute-start | bytes 4688 | tf_op jit(solution)/shard_map/ppermute | solution.py:23
  211.4 7.7 %collective-permute-start.21 = (f32[3,130,1]{2,1,0:T(8,128)S(1)}, f32[3,130,1]{2,1,0:T(8,128)S(1)}, u32[]{:S(2)}, u32[]{:S(2)}) collective-permute-start(f32[3,130,1]{2,1,0:T(8,128)S(1)} %get-tuple-element.185), channel_id=1, source_target_pairs={{2,0},{4,2},{6,4},{3,1},{5,3},{7,5},{10,8},{12,10},{14,12},{11,9},... | collective-permute-start | bytes 4688 | tf_op jit(solution)/shard_map/ppermute | solution.py:24
  219.4 4.6 %collective-permute-start.23 = (f32[1,130,514]{2,1,0:T(8,128)S(1)}, f32[1,130,514]{2,1,0:T(8,128)S(1)}, u32[]{:S(2)}, u32[]{:S(2)}) collective-permute-start(f32[1,130,514]{2,1,0:T(8,128)S(1)} %get-tuple-element.174), channel_id=1, source_target_pairs={{1,0},{3,2},{5,4},{7,6},{9,8},{11,10},{13,12},{15,14},{17,16},{19,... | collective-permute-start | bytes 801848 | tf_op jit(solution)/shard_map/ppermute | solution.py:24
  220.9 4.3 %collective-permute-start.24 = (f32[1,130,514]{2,1,0:T(8,128)S(1)}, f32[1,130,514]{2,1,0:T(8,128)S(1)}, u32[]{:S(2)}, u32[]{:S(2)}) collective-permute-start(f32[1,130,514]{2,1,0:T(8,128)S(1)} %get-tuple-element.175), channel_id=1, source_target_pairs={{0,1},{2,3},{4,5},{6,7},{8,9},{10,11},{12,13},{14,15},{16,17},{18,... | collective-permute-start | bytes 801848 | tf_op jit(solution)/shard_map/ppermute | solution.py:23
  275.9 28.6 %copy-start.3 = (f32[3,128,512]{2,1,0:T(8,128)S(1)}, f32[3,128,512]{2,1,0:T(8,128)}, u32[]{:S(2)}) copy-start(f32[3,128,512]{2,1,0:T(8,128)} %copy-done.2) | copy-start | bytes 2359300
  275.9 28.6 %copy-start.5 = (f32[3,128,512]{2,1,0:T(8,128)S(1)}, f32[3,128,512]{2,1,0:T(8,128)}, u32[]{:S(2)}) copy-start(f32[3,128,512]{2,1,0:T(8,128)} %copy-done.4) | copy-start | bytes 2359300
  278.0 32.5 %copy-start.1 = (f32[3,128,512]{2,1,0:T(8,128)}, f32[3,128,512]{2,1,0:T(8,128)S(1)}, u32[]{:S(2)}) copy-start(f32[3,128,512]{2,1,0:T(8,128)S(1)} %get-tuple-element.159) | copy-start | bytes 2359300
  278.0 32.5 %copy-start.8 = (f32[3,128,512]{2,1,0:T(8,128)}, f32[3,128,512]{2,1,0:T(8,128)S(1)}, u32[]{:S(2)}) copy-start(f32[3,128,512]{2,1,0:T(8,128)S(1)} %get-tuple-element.160) | copy-start | bytes 2359300
  278.0 5.5 %collective-permute-start.26 = (f32[3,1,512]{2,1,0:T(1,128)S(1)}, f32[3,1,512]{2,1,0:T(1,128)S(1)}, u32[]{:S(2)}, u32[]{:S(2)}) collective-permute-start(f32[3,1,512]{2,1,0:T(1,128)S(1)} %get-tuple-element.192), channel_id=1, source_target_pairs={{0,8},{8,16},{16,24},{1,9},{9,17},{17,25},{2,10},{10,18},{18,26},{... | collective-permute-start | bytes 18440 | tf_op jit(solution)/shard_map/ppermute | solution.py:23
  282.2 5.5 %collective-permute-start.25 = (f32[3,1,512]{2,1,0:T(1,128)S(1)}, f32[3,1,512]{2,1,0:T(1,128)S(1)}, u32[]{:S(2)}, u32[]{:S(2)}) collective-permute-start(f32[3,1,512]{2,1,0:T(1,128)S(1)} %get-tuple-element.193), channel_id=1, source_target_pairs={{8,0},{16,8},{24,16},{9,1},{17,9},{25,17},{10,2},{18,10},{26,18},{... | collective-permute-start | bytes 18440 | tf_op jit(solution)/shard_map/ppermute | solution.py:24
  287.9 6.3 %collective-permute-start.28 = (f32[3,130,1]{2,1,0:T(8,128)S(1)}, f32[3,130,1]{2,1,0:T(8,128)S(1)}, u32[]{:S(2)}, u32[]{:S(2)}) collective-permute-start(f32[3,130,1]{2,1,0:T(8,128)S(1)} %get-tuple-element.182), channel_id=1, source_target_pairs={{0,2},{2,4},{4,6},{1,3},{3,5},{5,7},{8,10},{10,12},{12,14},{9,11},... | collective-permute-start | bytes 4688 | tf_op jit(solution)/shard_map/ppermute | solution.py:23
  290.9 7.7 %collective-permute-start.27 = (f32[3,130,1]{2,1,0:T(8,128)S(1)}, f32[3,130,1]{2,1,0:T(8,128)S(1)}, u32[]{:S(2)}, u32[]{:S(2)}) collective-permute-start(f32[3,130,1]{2,1,0:T(8,128)S(1)} %get-tuple-element.183), channel_id=1, source_target_pairs={{2,0},{4,2},{6,4},{3,1},{5,3},{7,5},{10,8},{12,10},{14,12},{11,9},... | collective-permute-start | bytes 4688 | tf_op jit(solution)/shard_map/ppermute | solution.py:24
  298.9 4.4 %collective-permute-start.29 = (f32[1,130,514]{2,1,0:T(8,128)S(1)}, f32[1,130,514]{2,1,0:T(8,128)S(1)}, u32[]{:S(2)}, u32[]{:S(2)}) collective-permute-start(f32[1,130,514]{2,1,0:T(8,128)S(1)} %get-tuple-element.172), channel_id=1, source_target_pairs={{1,0},{3,2},{5,4},{7,6},{9,8},{11,10},{13,12},{15,14},{17,16},{19,... | collective-permute-start | bytes 801848 | tf_op jit(solution)/shard_map/ppermute | solution.py:24
  300.2 4.3 %collective-permute-start.30 = (f32[1,130,514]{2,1,0:T(8,128)S(1)}, f32[1,130,514]{2,1,0:T(8,128)S(1)}, u32[]{:S(2)}, u32[]{:S(2)}) collective-permute-start(f32[1,130,514]{2,1,0:T(8,128)S(1)} %get-tuple-element.173), channel_id=1, source_target_pairs={{0,1},{2,3},{4,5},{6,7},{8,9},{10,11},{12,13},{14,15},{16,17},{18,... | collective-permute-start | bytes 801848 | tf_op jit(solution)/shard_map/ppermute | solution.py:23
where the time goes:
time: 361 us; the launch traced here: 358 us
  blocking collectives  120 us (33%)
  starting transfers between devices  107 us (30%)
  waiting for transfers between devices  64 us (18%)
  other arithmetic  39.6 us (11%)
  matrix products  13.2 us (4%)
  between operations  11.5 us (3%)
    psum x3, blocking collectives, both_sums(): lax.psum((jnp.sum(residual * scaled), jnp.sum(scaled * image)), ('gx', 'g...  120 us
    ppermute x15, starting transfers between devices, with_halo(): before = lax.ppermute(last, axis, up)  85.9 us
    ppermute x15, waiting for transfers between devices, with_halo(): after = lax.ppermute(first, axis, down)  53.6 us
    ppermute x15, starting transfers between devices, with_halo(): after = lax.ppermute(first, axis, down)  19.6 us
    reduce_sum x3, other arithmetic, both_sums(): jnp.sum(scaled * image)  17.3 us
    ppermute x15, waiting for transfers between devices, with_halo(): before = lax.ppermute(last, axis, up)  10.4 us
    div x3, other arithmetic, solve(): scaled = residual / diagonal  7.49 us
  transfers between devices with their start and end apart: 31, of which 14 were waited for; matrix products, arithmetic and copies ran while one was open for 7% of the time, Pallas kernels for 0%

commit v1 on v0

--- a/solution.py
+++ b/solution.py
@@ -58,7 +58,9 @@
 
 
 def both_sums(residual, scaled, image):
-    return lax.psum((jnp.sum(residual * scaled), jnp.sum(scaled * image)), ("gx", "gy", "layer"))
+    return lax.psum(
+        lax.psum((jnp.sum(residual * scaled), jnp.sum(scaled * image)), "gx"), ("gy", "layer")
+    )
 
 
 def solve(apply, diagonal, rhs, start):

time: 361 us -> 312 us (0.86)
  blocking collectives: 120 us -> 75.3 us
  starting transfers between devices: 107 us -> 99.1 us
    psum x3 -> x6, blocking collectives: 120 us -> 75.3 us  [the longest x3 42.7 us: both_sums(): lax.psum(lax.psum((jnp.sum(residual * scaled), jnp.sum(scaled * image)),...]
    ppermute x15, starting transfers between devices: 85.9 us -> 78.4 us  [with_halo(): before = lax.ppermute(last, axis, up)]
  transfers between devices with their start and end apart: 31 -> 31, of which waited for: 14 -> 14; matrix products, arithmetic and copies ran while one was open for 7% -> 8% of each run, Pallas kernels for 0% -> 0%
where the time goes in v1:
time: 312 us; the launch traced here: 310 us
  starting transfers between devices  99.1 us (32%)
  blocking collectives  75.3 us (24%)
  waiting for transfers between devices  66.1 us (21%)
  other arithmetic  41.7 us (13%)
  matrix products  13.2 us (4%)
  between operations  11.1 us (4%)
    ppermute x15, starting transfers between devices, with_halo(): before = lax.ppermute(last, axis, up)  78.4 us
    ppermute x15, waiting for transfers between devices, with_halo(): after = lax.ppermute(first, axis, down)  55.4 us
    psum x3, blocking collectives, both_sums(): lax.psum(lax.psum((jnp.sum(residual * scaled), jnp.sum(scaled * image)),...  42.7 us
    psum x3, blocking collectives, both_sums(): lax.psum((jnp.sum(residual * scaled), jnp.sum(scaled * image)), 'gx')  32.5 us
    ppermute x15, starting transfers between devices, with_halo(): after = lax.ppermute(first, axis, down)  19.4 us
    reduce_sum x3, other arithmetic, both_sums(): jnp.sum(scaled * image)  17.2 us
    ppermute x15, waiting for transfers between devices, with_halo(): before = lax.ppermute(last, axis, up)  10.8 us
    div x3, other arithmetic, solve(): scaled = residual / diagonal  9.78 us
  transfers between devices with their start and end apart: 31, of which 14 were waited for; matrix products, arithmetic and copies ran while one was open for 8% of the time, Pallas kernels for 0%

profile of v1, /device:TPU:0, one launch (start us, length us, event | category | flops | bytes accessed | tf_op | source)
XLA Modules:
  0.0 309.7 jit_solution(3017599682625259105)
XLA Ops:
  1.5 4.9 %collective-permute-start.2 = (f32[3,1,512]{2,1,0:T(1,128)S(1)}, f32[3,1,512]{2,1,0:T(1,128)S(1)}, u32[]{:S(2)}, u32[]{:S(2)}) collective-permute-start(f32[3,1,512]{2,1,0:T(1,128)S(1)} %get-tuple-element.206), channel_id=1, source_target_pairs={{0,8},{8,16},{16,24},{1,9},{9,17},{17,25},{2,10},{10,18},{18,26},{... | collective-permute-start | bytes 18440 | tf_op jit(solution)/shard_map/ppermute | solution.py:23
  6.3 1.3 collective-permute-start.1
  8.5 4.5 %collective-permute-start.8 = (f32[3,1,512]{2,1,0:T(1,128)S(1)}, f32[3,1,512]{2,1,0:T(1,128)S(1)}, u32[]{:S(2)}, u32[]{:S(2)}) collective-permute-start(f32[3,1,512]{2,1,0:T(1,128)S(1)} %get-tuple-element.204), channel_id=1, source_target_pairs={{0,8},{8,16},{16,24},{1,9},{9,17},{17,25},{2,10},{10,18},{18,26},{... | collective-permute-start | bytes 18440 | tf_op jit(solution)/shard_map/ppermute | solution.py:23
  13.0 1.3 collective-permute-start.7
  15.7 5.8 %fusion.19 = f32[1,16384]{1,0:T(1,128)S(1)} fusion(bf16[256,1]{0,1:T(2,128)(2,1)S(1)} %reshape.111, bf16[1,1,16384,256]{3,2,1,0:T(8,128)(2,1)} %param.14), kind=kOutput, calls=%fused_computation.28 | convolution fusion | flops 8388608 | bytes 8454656 | tf_op jit(solution)/shard_map/dot_general | solution.py:91
  21.5 12.7 %while.15 = (s32[]{:T(128)}, f32[128,512]{1,0:T(8,128)S(1)}, s32[]{:T(128)}, s32[16384]{0:T(1024)}, f32[16384]{0:T(1024)S(1)}, /*index=5*/s32[]{:T(128)}, s32[]{:T(128)}, s32[]{:T(128)}, s32[]{:T(128)}) while((s32[]{:T(128)}, f32[128,512]{1,0:T(8,128)S(1)}, s32[]{:T(128)}, s32[16384]{0:T(1024)}, f32[16384]{0:T(1024)S(1)}, ...), condition=%wide.region_1.2_spmd.clone, body=%wide.region_0.1_spmd.clone.sunk | while | flops 135407104 | bytes 1071251 | solution.py:116
  34.2 1.3 collective-permute-start
  35.7 22.6 %collective-permute-start.4 = (f32[3,130,1]{2,1,0:T(8,128)S(1)}, f32[3,130,1]{2,1,0:T(8,128)S(1)}, u32[]{:S(2)}, u32[]{:S(2)}) collective-permute-start(f32[3,130,1]{2,1,0:T(8,128)S(1)} %get-tuple-element.196), channel_id=1, source_target_pairs={{0,2},{2,4},{4,6},{1,3},{3,5},{5,7},{8,10},{10,12},{12,14},{9,11},... | collective-permute-start | bytes 4688 | tf_op jit(solution)/shard_map/ppermute | solution.py:23
  58.3 1.3 collective-permute-start.3
  59.8 21.1 %collective-permute-start.10 = (f32[3,130,1]{2,1,0:T(8,128)S(1)}, f32[3,130,1]{2,1,0:T(8,128)S(1)}, u32[]{:S(2)}, u32[]{:S(2)}) collective-permute-start(f32[3,130,1]{2,1,0:T(8,128)S(1)} %get-tuple-element.194), channel_id=1, source_target_pairs={{0,2},{2,4},{4,6},{1,3},{3,5},{5,7},{8,10},{10,12},{12,14},{9,11},... | collective-permute-start | bytes 4688 | tf_op jit(solution)/shard_map/ppermute | solution.py:23
  80.9 1.3 collective-permute-start.9
  82.2 2.4 collective-permute-done.3
  84.9 2.0 collective-permute-start.6
  87.0 1.3 collective-permute-start.5
  88.3 21.1 %collective-permute-done.9 = f32[3,130,1]{2,1,0:T(8,128)S(1)} collective-permute-done((f32[3,130,1]{2,1,0:T(8,128)S(1)}, f32[3,130,1]{2,1,0:T(8,128)S(1)}, u32[]{:S(2)}, u32[]{:S(2)}) %collective-permute-start.9) | collective-permute-done | bytes 1592 | tf_op jit(solution)/shard_map/ppermute | solution.py:24
  111.0 3.1 collective-permute-start.12
  114.1 3.5 %add_add_fusion = (f32[3,128,512]{2,1,0:T(8,128)S(1)}, f32[3,128,512]{2,1,0:T(8,128)S(1)}, f32[3,128,512]{2,1,0:T(8,128)S(1)}) fusion(f32[3,128,512]{2,1,0:T(8,128)S(1)} %copy-done, f32[3,1,512]{2,1,0:T(1,128)S(1)} %collective-permute-done.1, f32[3,1,512]{2,1,0:T(1,128)S(1)} %collective-permute-done.2, f32[3,130,1]{2,1,0:T(8,128)S(1)} %collective-permute-done.3, ...), kind=kLoop, calls=%fused_computation.187 | loop fusion | flops 8650752 | bytes 3957840 | tf_op jit(solution)/shard_map/add | solution.py:46
  117.8 6.0 %fusion.83 = (f32[3,128,512]{2,1,0:T(8,128)S(1)}, f32[3,128,512]{2,1,0:T(8,128)S(1)}) fusion(f32[3,128,512]{2,1,0:T(8,128)S(1)} %fusion.76, f32[3,128,512]{2,1,0:T(8,128)S(1)} %get-tuple-element.175, f32[3,130,1]{2,1,0:T(8,128)S(1)} %collective-permute-done.9, f32[3,1,512]{2,1,0:T(1,128)S(1)} %collective-permute-done.7, f32[3,128,512]{2,1,0:T(8,128)} %param.21, ...), kind=kLoop, calls=%fused_computation.238 | loop fusion | flops 10616832 | bytes 6332544 | tf_op jit(solution)/shard_map/div | solution.py:69
  125.1 1.3 collective-permute-start.13
  126.4 8.7 %collective-permute-done.13 = f32[3,1,512]{2,1,0:T(1,128)S(1)} collective-permute-done((f32[3,1,512]{2,1,0:T(1,128)S(1)}, f32[3,1,512]{2,1,0:T(1,128)S(1)}, u32[]{:S(2)}, u32[]{:S(2)}) %collective-permute-start.13) | collective-permute-done | bytes 6176 | tf_op jit(solution)/shard_map/ppermute | solution.py:24
  135.3 3.7 %collective-permute-start.16 = (f32[3,130,1]{2,1,0:T(8,128)S(1)}, f32[3,130,1]{2,1,0:T(8,128)S(1)}, u32[]{:S(2)}, u32[]{:S(2)}) collective-permute-start(f32[3,130,1]{2,1,0:T(8,128)S(1)} %get-tuple-element.192), channel_id=1, source_target_pairs={{0,2},{2,4},{4,6},{1,3},{3,5},{5,7},{8,10},{10,12},{12,14},{9,11},... | collective-permute-start | bytes 4688 | tf_op jit(solution)/shard_map/ppermute | solution.py:23
  140.3 2.6 collective-permute-done.16
  142.9 4.1 %collective-permute-done.15 = f32[3,130,1]{2,1,0:T(8,128)S(1)} collective-permute-done((f32[3,130,1]{2,1,0:T(8,128)S(1)}, f32[3,130,1]{2,1,0:T(8,128)S(1)}, u32[]{:S(2)}, u32[]{:S(2)}) %collective-permute-start.15) | collective-permute-done | bytes 1592 | tf_op jit(solution)/shard_map/ppermute | solution.py:24
  148.7 3.1 collective-permute-start.18
  153.0 5.0 %multiply_reduce_fusion.4 = (f32[]{:T(128)}, f32[]{:T(128)}, f32[3,128,512]{2,1,0:T(8,128)}) fusion(f32[3,128,512]{2,1,0:T(8,128)S(1)} %get-tuple-element.171, f32[3,128,512]{2,1,0:T(8,128)S(1)} %get-tuple-element.172, f32[3,128,512]{2,1,0:T(8,128)S(1)} %get-tuple-element.175, f32[3,130,1]{2,1,0:T(8,128)S(1)} %collective-permute-done.15, ...), kind=kLoop, calls=%fused_computation.184 | loop fusion | flops 11010046 | bytes 6070408 | tf_op jit(solution)/shard_map/reduce_sum | solution.py:62
  158.0 10.6 %all-reduce.6 = (f32[]{:T(128)}, f32[]{:T(128)}) all-reduce(f32[]{:T(128)} %get-tuple-element.141, f32[]{:T(128)} %get-tuple-element.140), channel_id=1, replica_groups=mesh['gx'=4,'gy'=4,'layer'=2] {'gx'}, use_global_device_ids=true, to_apply=%region_3.4 | all-reduce | flops 2 | bytes 16 | tf_op jit(solution)/shard_map/psum | solution.py:62
  168.6 14.2 %all-reduce.3 = (f32[]{:T(128)}, f32[]{:T(128)}) all-reduce(f32[]{:T(128)} %get-tuple-element.162, f32[]{:T(128)} %get-tuple-element.163), channel_id=1, replica_groups=mesh['gx'=4,'gy'=4,'layer'=2] {'gy','layer'}, use_global_device_ids=true, to_apply=%region_4.5 | all-reduce | flops 2 | bytes 16 | tf_op jit(solution)/shard_map/psum | solution.py:61
  184.0 1.7 fusion.81
  185.7 1.6 collective-permute-start.20
  188.7 5.4 %collective-permute-done.19 = f32[3,1,512]{2,1,0:T(1,128)S(1)} collective-permute-done((f32[3,1,512]{2,1,0:T(1,128)S(1)}, f32[3,1,512]{2,1,0:T(1,128)S(1)}, u32[]{:S(2)}, u32[]{:S(2)}) %collective-permute-start.19) | collective-permute-done | bytes 6176 | tf_op jit(solution)/shard_map/ppermute | solution.py:24
  194.2 1.3 collective-permute-start.22
  196.8 2.3 collective-permute-done.22
  199.1 4.1 %collective-permute-done.21 = f32[3,130,1]{2,1,0:T(8,128)S(1)} collective-permute-done((f32[3,130,1]{2,1,0:T(8,128)S(1)}, f32[3,130,1]{2,1,0:T(8,128)S(1)}, u32[]{:S(2)}, u32[]{:S(2)}) %collective-permute-start.21) | collective-permute-done | bytes 1592 | tf_op jit(solution)/shard_map/ppermute | solution.py:24
  204.9 3.2 %collective-permute-start.24 = (f32[1,130,514]{2,1,0:T(8,128)S(1)}, f32[1,130,514]{2,1,0:T(8,128)S(1)}, u32[]{:S(2)}, u32[]{:S(2)}) collective-permute-start(f32[1,130,514]{2,1,0:T(8,128)S(1)} %get-tuple-element.181), channel_id=1, source_target_pairs={{0,1},{2,3},{4,5},{6,7},{8,9},{10,11},{12,13},{14,15},{16,17},{18,... | collective-permute-start | bytes 801848 | tf_op jit(solution)/shard_map/ppermute | solution.py:23
  209.2 6.3 %multiply_reduce_fusion.2 = (f32[]{:T(128)}, f32[]{:T(128)}, f32[3,128,512]{2,1,0:T(8,128)}) fusion(f32[3,128,512]{2,1,0:T(8,128)S(1)} %get-tuple-element.168, f32[3,128,512]{2,1,0:T(8,128)S(1)} %get-tuple-element.169, f32[3,128,512]{2,1,0:T(8,128)} %copy-done.4, f32[3,130,1]{2,1,0:T(8,128)S(1)} %collective-permute-done.21, ...), kind=kLoop, calls=%fused_computation.181 | loop fusion | flops 11010046 | bytes 6070408 | tf_op jit(solution)/shard_map/reduce_sum | solution.py:62
  215.5 11.0 %all-reduce.5 = (f32[]{:T(128)}, f32[]{:T(128)}) all-reduce(f32[]{:T(128)} %get-tuple-element.139, f32[]{:T(128)} %get-tuple-element.138), channel_id=1, replica_groups=mesh['gx'=4,'gy'=4,'layer'=2] {'gx'}, use_global_device_ids=true, to_apply=%region_9.10 | all-reduce | flops 2 | bytes 16 | tf_op jit(solution)/shard_map/psum | solution.py:62
  226.5 14.2 %all-reduce.2 = (f32[]{:T(128)}, f32[]{:T(128)}) all-reduce(f32[]{:T(128)} %get-tuple-element.160, f32[]{:T(128)} %get-tuple-element.161), channel_id=1, replica_groups=mesh['gx'=4,'gy'=4,'layer'=2] {'gy','layer'}, use_global_device_ids=true, to_apply=%region_10.11 | all-reduce | flops 2 | bytes 16 | tf_op jit(solution)/shard_map/psum | solution.py:61
  244.9 2.1 fusion.79
  247.1 1.6 collective-permute-start.26
  250.1 5.4 %collective-permute-done.25 = f32[3,1,512]{2,1,0:T(1,128)S(1)} collective-permute-done((f32[3,1,512]{2,1,0:T(1,128)S(1)}, f32[3,1,512]{2,1,0:T(1,128)S(1)}, u32[]{:S(2)}, u32[]{:S(2)}) %collective-permute-start.25) | collective-permute-done | bytes 6176 | tf_op jit(solution)/shard_map/ppermute | solution.py:24
  255.6 1.3 collective-permute-start.28
  258.2 2.3 collective-permute-done.28
  260.4 4.1 %collective-permute-done.27 = f32[3,130,1]{2,1,0:T(8,128)S(1)} collective-permute-done((f32[3,130,1]{2,1,0:T(8,128)S(1)}, f32[3,130,1]{2,1,0:T(8,128)S(1)}, u32[]{:S(2)}, u32[]{:S(2)}) %collective-permute-start.27) | collective-permute-done | bytes 1592 | tf_op jit(solution)/shard_map/ppermute | solution.py:24
  266.2 3.1 collective-permute-start.30
  270.5 6.0 %multiply_reduce_fusion = (f32[]{:T(128)}, f32[]{:T(128)}, f32[3,128,512]{2,1,0:T(8,128)}) fusion(f32[3,128,512]{2,1,0:T(8,128)S(1)} %get-tuple-element.165, f32[3,128,512]{2,1,0:T(8,128)S(1)} %get-tuple-element.166, f32[3,128,512]{2,1,0:T(8,128)S(1)} %copy-done.5, f32[3,130,1]{2,1,0:T(8,128)S(1)} %collective-permute-done.27, ...), kind=kLoop, calls=%fused_computation.177 | loop fusion | flops 11010046 | bytes 6070408 | tf_op jit(solution)/shard_map/reduce_sum | solution.py:62
  276.5 10.9 %all-reduce.4 = (f32[]{:T(128)}, f32[]{:T(128)}) all-reduce(f32[]{:T(128)} %get-tuple-element.137, f32[]{:T(128)} %get-tuple-element.136), channel_id=1, replica_groups=mesh['gx'=4,'gy'=4,'layer'=2] {'gx'}, use_global_device_ids=true, to_apply=%region_15.16 | all-reduce | flops 2 | bytes 16 | tf_op jit(solution)/shard_map/psum | solution.py:62
  287.4 14.3 %all-reduce.1 = (f32[]{:T(128)}, f32[]{:T(128)}) all-reduce(f32[]{:T(128)} %get-tuple-element.158, f32[]{:T(128)} %get-tuple-element.159), channel_id=1, replica_groups=mesh['gx'=4,'gy'=4,'layer'=2] {'gy','layer'}, use_global_device_ids=true, to_apply=%region_16.17 | all-reduce | flops 2 | bytes 16 | tf_op jit(solution)/shard_map/psum | solution.py:61
  305.4 4.2 %multiply_subtract_fusion = (f32[3,128,512]{2,1,0:T(8,128)}, f32[3,128,512]{2,1,0:T(8,128)}) fusion(f32[3,128,512]{2,1,0:T(8,128)} %copy-done.8, f32[3,128,512]{2,1,0:T(8,128)} %get-tuple-element.164, f32[]{:T(128)S(6)} %div.84, f32[]{:T(128)S(6)} %div.86, f32[3,128,512]{2,1,0:T(8,128)} %get-tuple-element.167, f32[3,128,512]{2,1,0:T(8,128)} %get-tuple-element.170, ...), kind=kLoop, calls=%fused_computation.175 | loop fusion | flops 3145728 | bytes 7864340 | tf_op jit(solution)/shard_map/sub | solution.py:76
  (96 shorter events, 33.9 us)
Async XLA Ops:
  1.5 34.1 %collective-permute-start.2 = (f32[3,1,512]{2,1,0:T(1,128)S(1)}, f32[3,1,512]{2,1,0:T(1,128)S(1)}, u32[]{:S(2)}, u32[]{:S(2)}) collective-permute-start(f32[3,1,512]{2,1,0:T(1,128)S(1)} %get-tuple-element.206), channel_id=1, source_target_pairs={{0,8},{8,16},{16,24},{1,9},{9,17},{17,25},{2,10},{10,18},{18,26},{... | collective-permute-start | bytes 18440 | tf_op jit(solution)/shard_map/ppermute | solution.py:23
  6.3 29.2 %collective-permute-start.1 = (f32[3,1,512]{2,1,0:T(1,128)S(1)}, f32[3,1,512]{2,1,0:T(1,128)S(1)}, u32[]{:S(2)}, u32[]{:S(2)}) collective-permute-start(f32[3,1,512]{2,1,0:T(1,128)S(1)} %get-tuple-element.207), channel_id=1, source_target_pairs={{8,0},{16,8},{24,16},{9,1},{17,9},{25,17},{10,2},{18,10},{26,18},{... | collective-permute-start | bytes 18440 | tf_op jit(solution)/shard_map/ppermute | solution.py:24
  8.5 51.1 %collective-permute-start.8 = (f32[3,1,512]{2,1,0:T(1,128)S(1)}, f32[3,1,512]{2,1,0:T(1,128)S(1)}, u32[]{:S(2)}, u32[]{:S(2)}) collective-permute-start(f32[3,1,512]{2,1,0:T(1,128)S(1)} %get-tuple-element.204), channel_id=1, source_target_pairs={{0,8},{8,16},{16,24},{1,9},{9,17},{17,25},{2,10},{10,18},{18,26},{... | collective-permute-start | bytes 18440 | tf_op jit(solution)/shard_map/ppermute | solution.py:23
  13.0 46.6 %collective-permute-start.7 = (f32[3,1,512]{2,1,0:T(1,128)S(1)}, f32[3,1,512]{2,1,0:T(1,128)S(1)}, u32[]{:S(2)}, u32[]{:S(2)}) collective-permute-start(f32[3,1,512]{2,1,0:T(1,128)S(1)} %get-tuple-element.205), channel_id=1, source_target_pairs={{8,0},{16,8},{24,16},{9,1},{17,9},{25,17},{10,2},{18,10},{26,18},{... | collective-permute-start | bytes 18440 | tf_op jit(solution)/shard_map/ppermute | solution.py:24
  15.7 19.9 %copy-start = (f32[3,128,512]{2,1,0:T(8,128)S(1)}, f32[3,128,512]{2,1,0:T(8,128)}, u32[]{:S(2)}) copy-start(f32[3,128,512]{2,1,0:T(8,128)} %param.18) | copy-start | bytes 2359300
  15.7 44.0 %copy-start.6 = (f32[3,128,512]{2,1,0:T(8,128)S(1)}, f32[3,128,512]{2,1,0:T(8,128)}, u32[]{:S(2)}) copy-start(f32[3,128,512]{2,1,0:T(8,128)} %param.21) | copy-start | bytes 2359300
  34.2 79.8 %collective-permute-start = (f32[128,512]{1,0:T(8,128)S(1)}, f32[128,512]{1,0:T(8,128)S(1)}, u32[]{:S(2)}, u32[]{:S(2)}) collective-permute-start(f32[128,512]{1,0:T(8,128)S(1)} %get-tuple-element.121), channel_id=1, source_target_pairs={{1,0},{3,2},{5,4},{7,6},{9,8},{11,10},{13,12},{15,14},{17,16},{19,... | collective-permute-start | bytes 786440 | tf_op jit(solution)/shard_map/ppermute | solution.py:13
  35.7 46.5 %collective-permute-start.4 = (f32[3,130,1]{2,1,0:T(8,128)S(1)}, f32[3,130,1]{2,1,0:T(8,128)S(1)}, u32[]{:S(2)}, u32[]{:S(2)}) collective-permute-start(f32[3,130,1]{2,1,0:T(8,128)S(1)} %get-tuple-element.196), channel_id=1, source_target_pairs={{0,2},{2,4},{4,6},{1,3},{3,5},{5,7},{8,10},{10,12},{12,14},{9,11},... | collective-permute-start | bytes 4688 | tf_op jit(solution)/shard_map/ppermute | solution.py:23
  58.3 26.3 %collective-permute-start.3 = (f32[3,130,1]{2,1,0:T(8,128)S(1)}, f32[3,130,1]{2,1,0:T(8,128)S(1)}, u32[]{:S(2)}, u32[]{:S(2)}) collective-permute-start(f32[3,130,1]{2,1,0:T(8,128)S(1)} %get-tuple-element.197), channel_id=1, source_target_pairs={{2,0},{4,2},{6,4},{3,1},{5,3},{7,5},{10,8},{12,10},{14,12},{11,9},... | collective-permute-start | bytes 4688 | tf_op jit(solution)/shard_map/ppermute | solution.py:24
  59.8 28.5 %collective-permute-start.10 = (f32[3,130,1]{2,1,0:T(8,128)S(1)}, f32[3,130,1]{2,1,0:T(8,128)S(1)}, u32[]{:S(2)}, u32[]{:S(2)}) collective-permute-start(f32[3,130,1]{2,1,0:T(8,128)S(1)} %get-tuple-element.194), channel_id=1, source_target_pairs={{0,2},{2,4},{4,6},{1,3},{3,5},{5,7},{8,10},{10,12},{12,14},{9,11},... | collective-permute-start | bytes 4688 | tf_op jit(solution)/shard_map/ppermute | solution.py:23
  80.9 28.5 %collective-permute-start.9 = (f32[3,130,1]{2,1,0:T(8,128)S(1)}, f32[3,130,1]{2,1,0:T(8,128)S(1)}, u32[]{:S(2)}, u32[]{:S(2)}) collective-permute-start(f32[3,130,1]{2,1,0:T(8,128)S(1)} %get-tuple-element.195), channel_id=1, source_target_pairs={{2,0},{4,2},{6,4},{3,1},{5,3},{7,5},{10,8},{12,10},{14,12},{11,9},... | collective-permute-start | bytes 4688 | tf_op jit(solution)/shard_map/ppermute | solution.py:24
  84.6 68.4 %copy-start.7 = (f32[3,130,1]{2,1,0:T(8,128)}, f32[3,130,1]{2,1,0:T(8,128)S(1)}, u32[]{:S(2)}) copy-start(f32[3,130,1]{2,1,0:T(8,128)S(1)} %collective-permute-done.3) | copy-start | bytes 4684
  84.9 29.2 %collective-permute-start.6 = (f32[1,130,514]{2,1,0:T(8,128)S(1)}, f32[1,130,514]{2,1,0:T(8,128)S(1)}, u32[]{:S(2)}, u32[]{:S(2)}) collective-permute-start(f32[1,130,514]{2,1,0:T(8,128)S(1)} %get-tuple-element.186), channel_id=1, source_target_pairs={{0,1},{2,3},{4,5},{6,7},{8,9},{10,11},{12,13},{14,15},{16,17},{18,... | collective-permute-start | bytes 801848 | tf_op jit(solution)/shard_map/ppermute | solution.py:23
  87.0 27.1 %collective-permute-start.5 = (f32[1,130,514]{2,1,0:T(8,128)S(1)}, f32[1,130,514]{2,1,0:T(8,128)S(1)}, u32[]{:S(2)}, u32[]{:S(2)}) collective-permute-start(f32[1,130,514]{2,1,0:T(8,128)S(1)} %get-tuple-element.187), channel_id=1, source_target_pairs={{1,0},{3,2},{5,4},{7,6},{9,8},{11,10},{13,12},{15,14},{17,16},{19,... | collective-permute-start | bytes 801848 | tf_op jit(solution)/shard_map/ppermute | solution.py:24
  109.7 8.1 %collective-permute-start.11 = (f32[1,130,514]{2,1,0:T(8,128)S(1)}, f32[1,130,514]{2,1,0:T(8,128)S(1)}, u32[]{:S(2)}, u32[]{:S(2)}) collective-permute-start(f32[1,130,514]{2,1,0:T(8,128)S(1)} %get-tuple-element.184), channel_id=1, source_target_pairs={{1,0},{3,2},{5,4},{7,6},{9,8},{11,10},{13,12},{15,14},{17,16},{19,... | collective-permute-start | bytes 801848 | tf_op jit(solution)/shard_map/ppermute | solution.py:24
  111.0 6.8 %collective-permute-start.12 = (f32[1,130,514]{2,1,0:T(8,128)S(1)}, f32[1,130,514]{2,1,0:T(8,128)S(1)}, u32[]{:S(2)}, u32[]{:S(2)}) collective-permute-start(f32[1,130,514]{2,1,0:T(8,128)S(1)} %get-tuple-element.185), channel_id=1, source_target_pairs={{0,1},{2,3},{4,5},{6,7},{8,9},{10,11},{12,13},{14,15},{16,17},{18,... | collective-permute-start | bytes 801848 | tf_op jit(solution)/shard_map/ppermute | solution.py:23
  117.6 40.3 %copy-start.2 = (f32[3,128,512]{2,1,0:T(8,128)}, f32[3,128,512]{2,1,0:T(8,128)S(1)}, u32[]{:S(2)}) copy-start(f32[3,128,512]{2,1,0:T(8,128)S(1)} %get-tuple-element.174) | copy-start | bytes 2359300
  117.6 40.3 %copy-start.4 = (f32[3,128,512]{2,1,0:T(8,128)}, f32[3,128,512]{2,1,0:T(8,128)S(1)}, u32[]{:S(2)}) copy-start(f32[3,128,512]{2,1,0:T(8,128)S(1)} %get-tuple-element.175) | copy-start | bytes 2359300
  123.8 34.2 %copy-start.10 = (f32[3,128,512]{2,1,0:T(8,128)}, f32[3,128,512]{2,1,0:T(8,128)S(1)}, u32[]{:S(2)}) copy-start(f32[3,128,512]{2,1,0:T(8,128)S(1)} %get-tuple-element.172) | copy-start | bytes 2359300
  123.8 2.6 collective-permute-start.14
  125.1 10.1 %collective-permute-start.13 = (f32[3,1,512]{2,1,0:T(1,128)S(1)}, f32[3,1,512]{2,1,0:T(1,128)S(1)}, u32[]{:S(2)}, u32[]{:S(2)}) collective-permute-start(f32[3,1,512]{2,1,0:T(1,128)S(1)} %get-tuple-element.203), channel_id=1, source_target_pairs={{8,0},{16,8},{24,16},{9,1},{17,9},{25,17},{10,2},{18,10},{26,18},{... | collective-permute-start | bytes 18440 | tf_op jit(solution)/shard_map/ppermute | solution.py:24
  135.3 7.6 %collective-permute-start.16 = (f32[3,130,1]{2,1,0:T(8,128)S(1)}, f32[3,130,1]{2,1,0:T(8,128)S(1)}, u32[]{:S(2)}, u32[]{:S(2)}) collective-permute-start(f32[3,130,1]{2,1,0:T(8,128)S(1)} %get-tuple-element.192), channel_id=1, source_target_pairs={{0,2},{2,4},{4,6},{1,3},{3,5},{5,7},{8,10},{10,12},{12,14},{9,11},... | collective-permute-start | bytes 4688 | tf_op jit(solution)/shard_map/ppermute | solution.py:23
  139.0 8.0 %collective-permute-start.15 = (f32[3,130,1]{2,1,0:T(8,128)S(1)}, f32[3,130,1]{2,1,0:T(8,128)S(1)}, u32[]{:S(2)}, u32[]{:S(2)}) collective-permute-start(f32[3,130,1]{2,1,0:T(8,128)S(1)} %get-tuple-element.193), channel_id=1, source_target_pairs={{2,0},{4,2},{6,4},{3,1},{5,3},{7,5},{10,8},{12,10},{14,12},{11,9},... | collective-permute-start | bytes 4688 | tf_op jit(solution)/shard_map/ppermute | solution.py:24
  147.4 4.4 %collective-permute-start.17 = (f32[1,130,514]{2,1,0:T(8,128)S(1)}, f32[1,130,514]{2,1,0:T(8,128)S(1)}, u32[]{:S(2)}, u32[]{:S(2)}) collective-permute-start(f32[1,130,514]{2,1,0:T(8,128)S(1)} %get-tuple-element.182), channel_id=1, source_target_pairs={{1,0},{3,2},{5,4},{7,6},{9,8},{11,10},{13,12},{15,14},{17,16},{19,... | collective-permute-start | bytes 801848 | tf_op jit(solution)/shard_map/ppermute | solution.py:24
  148.7 4.3 %collective-permute-start.18 = (f32[1,130,514]{2,1,0:T(8,128)S(1)}, f32[1,130,514]{2,1,0:T(8,128)S(1)}, u32[]{:S(2)}, u32[]{:S(2)}) collective-permute-start(f32[1,130,514]{2,1,0:T(8,128)S(1)} %get-tuple-element.183), channel_id=1, source_target_pairs={{0,1},{2,3},{4,5},{6,7},{8,9},{10,11},{12,13},{14,15},{16,17},{18,... | collective-permute-start | bytes 801848 | tf_op jit(solution)/shard_map/ppermute | solution.py:23
  185.7 23.5 %copy-start.9 = (f32[3,128,512]{2,1,0:T(8,128)}, f32[3,128,512]{2,1,0:T(8,128)S(1)}, u32[]{:S(2)}) copy-start(f32[3,128,512]{2,1,0:T(8,128)S(1)} %get-tuple-element.169) | copy-start | bytes 2359300
  185.7 3.0 collective-permute-start.20
  187.4 6.7 %collective-permute-start.19 = (f32[3,1,512]{2,1,0:T(1,128)S(1)}, f32[3,1,512]{2,1,0:T(1,128)S(1)}, u32[]{:S(2)}, u32[]{:S(2)}) collective-permute-start(f32[3,1,512]{2,1,0:T(1,128)S(1)} %get-tuple-element.201), channel_id=1, source_target_pairs={{8,0},{16,8},{24,16},{9,1},{17,9},{25,17},{10,2},{18,10},{26,18},{... | collective-permute-start | bytes 18440 | tf_op jit(solution)/shard_map/ppermute | solution.py:24
  194.2 4.9 %collective-permute-start.22 = (f32[3,130,1]{2,1,0:T(8,128)S(1)}, f32[3,130,1]{2,1,0:T(8,128)S(1)}, u32[]{:S(2)}, u32[]{:S(2)}) collective-permute-start(f32[3,130,1]{2,1,0:T(8,128)S(1)} %get-tuple-element.190), channel_id=1, source_target_pairs={{0,2},{2,4},{4,6},{1,3},{3,5},{5,7},{8,10},{10,12},{12,14},{9,11},... | collective-permute-start | bytes 4688 | tf_op jit(solution)/shard_map/ppermute | solution.py:23
  195.5 7.7 %collective-permute-start.21 = (f32[3,130,1]{2,1,0:T(8,128)S(1)}, f32[3,130,1]{2,1,0:T(8,128)S(1)}, u32[]{:S(2)}, u32[]{:S(2)}) collective-permute-start(f32[3,130,1]{2,1,0:T(8,128)S(1)} %get-tuple-element.191), channel_id=1, source_target_pairs={{2,0},{4,2},{6,4},{3,1},{5,3},{7,5},{10,8},{12,10},{14,12},{11,9},... | collective-permute-start | bytes 4688 | tf_op jit(solution)/shard_map/ppermute | solution.py:24
  203.6 4.6 %collective-permute-start.23 = (f32[1,130,514]{2,1,0:T(8,128)S(1)}, f32[1,130,514]{2,1,0:T(8,128)S(1)}, u32[]{:S(2)}, u32[]{:S(2)}) collective-permute-start(f32[1,130,514]{2,1,0:T(8,128)S(1)} %get-tuple-element.180), channel_id=1, source_target_pairs={{1,0},{3,2},{5,4},{7,6},{9,8},{11,10},{13,12},{15,14},{17,16},{19,... | collective-permute-start | bytes 801848 | tf_op jit(solution)/shard_map/ppermute | solution.py:24
  204.9 4.3 %collective-permute-start.24 = (f32[1,130,514]{2,1,0:T(8,128)S(1)}, f32[1,130,514]{2,1,0:T(8,128)S(1)}, u32[]{:S(2)}, u32[]{:S(2)}) collective-permute-start(f32[1,130,514]{2,1,0:T(8,128)S(1)} %get-tuple-element.181), channel_id=1, source_target_pairs={{0,1},{2,3},{4,5},{6,7},{8,9},{10,11},{12,13},{14,15},{16,17},{18,... | collective-permute-start | bytes 801848 | tf_op jit(solution)/shard_map/ppermute | solution.py:23
  244.9 25.6 %copy-start.3 = (f32[3,128,512]{2,1,0:T(8,128)S(1)}, f32[3,128,512]{2,1,0:T(8,128)}, u32[]{:S(2)}) copy-start(f32[3,128,512]{2,1,0:T(8,128)} %copy-done.2) | copy-start | bytes 2359300
  244.9 25.6 %copy-start.5 = (f32[3,128,512]{2,1,0:T(8,128)S(1)}, f32[3,128,512]{2,1,0:T(8,128)}, u32[]{:S(2)}) copy-start(f32[3,128,512]{2,1,0:T(8,128)} %copy-done.4) | copy-start | bytes 2359300
  247.0 29.5 %copy-start.1 = (f32[3,128,512]{2,1,0:T(8,128)}, f32[3,128,512]{2,1,0:T(8,128)S(1)}, u32[]{:S(2)}) copy-start(f32[3,128,512]{2,1,0:T(8,128)S(1)} %get-tuple-element.165) | copy-start | bytes 2359300
  247.1 29.5 %copy-start.8 = (f32[3,128,512]{2,1,0:T(8,128)}, f32[3,128,512]{2,1,0:T(8,128)S(1)}, u32[]{:S(2)}) copy-start(f32[3,128,512]{2,1,0:T(8,128)S(1)} %get-tuple-element.166) | copy-start | bytes 2359300
  247.1 3.0 collective-permute-start.26
  248.7 6.7 %collective-permute-start.25 = (f32[3,1,512]{2,1,0:T(1,128)S(1)}, f32[3,1,512]{2,1,0:T(1,128)S(1)}, u32[]{:S(2)}, u32[]{:S(2)}) collective-permute-start(f32[3,1,512]{2,1,0:T(1,128)S(1)} %get-tuple-element.199), channel_id=1, source_target_pairs={{8,0},{16,8},{24,16},{9,1},{17,9},{25,17},{10,2},{18,10},{26,18},{... | collective-permute-start | bytes 18440 | tf_op jit(solution)/shard_map/ppermute | solution.py:24
  255.6 4.9 %collective-permute-start.28 = (f32[3,130,1]{2,1,0:T(8,128)S(1)}, f32[3,130,1]{2,1,0:T(8,128)S(1)}, u32[]{:S(2)}, u32[]{:S(2)}) collective-permute-start(f32[3,130,1]{2,1,0:T(8,128)S(1)} %get-tuple-element.188), channel_id=1, source_target_pairs={{0,2},{2,4},{4,6},{1,3},{3,5},{5,7},{8,10},{10,12},{12,14},{9,11},... | collective-permute-start | bytes 4688 | tf_op jit(solution)/shard_map/ppermute | solution.py:23
  256.9 7.7 %collective-permute-start.27 = (f32[3,130,1]{2,1,0:T(8,128)S(1)}, f32[3,130,1]{2,1,0:T(8,128)S(1)}, u32[]{:S(2)}, u32[]{:S(2)}) collective-permute-start(f32[3,130,1]{2,1,0:T(8,128)S(1)} %get-tuple-element.189), channel_id=1, source_target_pairs={{2,0},{4,2},{6,4},{3,1},{5,3},{7,5},{10,8},{12,10},{14,12},{11,9},... | collective-permute-start | bytes 4688 | tf_op jit(solution)/shard_map/ppermute | solution.py:24
  264.9 4.4 %collective-permute-start.29 = (f32[1,130,514]{2,1,0:T(8,128)S(1)}, f32[1,130,514]{2,1,0:T(8,128)S(1)}, u32[]{:S(2)}, u32[]{:S(2)}) collective-permute-start(f32[1,130,514]{2,1,0:T(8,128)S(1)} %get-tuple-element.178), channel_id=1, source_target_pairs={{1,0},{3,2},{5,4},{7,6},{9,8},{11,10},{13,12},{15,14},{17,16},{19,... | collective-permute-start | bytes 801848 | tf_op jit(solution)/shard_map/ppermute | solution.py:24
  266.2 4.3 %collective-permute-start.30 = (f32[1,130,514]{2,1,0:T(8,128)S(1)}, f32[1,130,514]{2,1,0:T(8,128)S(1)}, u32[]{:S(2)}, u32[]{:S(2)}) collective-permute-start(f32[1,130,514]{2,1,0:T(8,128)S(1)} %get-tuple-element.179), channel_id=1, source_target_pairs={{0,1},{2,3},{4,5},{6,7},{8,9},{10,11},{12,13},{14,15},{16,17},{18,... | collective-permute-start | bytes 801848 | tf_op jit(solution)/shard_map/ppermute | solution.py:23
